TPU v7x, 32 devices: a whole 2x2x4 slice. The times are simulated.
32 devices in a mesh: freq: 8 (over z, core), plane: 4 (over y, x).
Axes of the slice: x: 2, y: 2, z: 4, core: 2. Of those that a mesh axis runs over, the one named last changes fastest.
Arguments:
- contrast: float32 [2, 512, 2, 512], P(None, 'plane'), may hold values from -1 to 1
- green_kernel: bfloat16 [8, 2, 2, 2, 512, 512], P('freq', None, None, None, 'plane'), may hold values from -1 to 1
- source_pos: int32 [8, 2], P('freq'), may hold values from 0 to 511
- receiver_pos: int32 [8, 2, 64], P('freq'), may hold values from 0 to 511
- measured: float32 [8, 2, 64], P('freq'), may hold values from -6 to 6
Outputs:
- new_contrast: float32 [2, 512, 2, 512], P(None, 'plane')
- new_field: float32 [8, 2, 512, 2, 512], P('freq', None, 'plane')
Inputs may be any that keep to these rules, and one draw needn't show every extreme that they name: `source_pos`: row 0 is the x index and row 1 the y index of the source cell in layer 0. `receiver_pos`: row 0 holds the x indices and row 1 the y indices of the receiver cells in layer 0; receivers may coincide.
All inputs are finite; a program needn't handle non-finite values.
Results may differ from a plain program's by a relative error of at most 0.02.
Values may be sent and summed in bfloat16 or wider, within the bound.
A program may use at most 64 MiB of HBM per device.

v0:
```python
import functools
import math

import jax
import numpy as np
import jax.numpy as jnp
from jax import lax
from jax.experimental import pallas as pl
from jax.experimental.pallas import tpu as pltpu
from jax.sharding import PartitionSpec as P

ITERS = 2


source_gain = 3.0


def phase_tables(length, out_type):
    positions = lax.iota(jnp.int32, length)
    turn_count = positions[:, None] * positions[None, :] % length
    angles = turn_count.astype(jnp.float32) * (2.0 * math.pi / length)
    norm_scale = 1.0 / math.sqrt(length)
    return jnp.concatenate(
        [jnp.cos(angles) * norm_scale, jnp.sin(angles) * norm_scale], axis=1
    ).astype(out_type)


def line_phase(positions, location, length):
    turn_count = positions * location % length
    angles = turn_count.astype(jnp.float32) * (2.0 * math.pi / length)
    return (jnp.cos(angles), -jnp.sin(angles))


def complex_product(first, second):
    return jnp.stack(
        [first[0] * second[0] - first[1] * second[1], first[0] * second[1] + first[1] * second[0]]
    )


def forward(wave_field, dft_table):
    row_count, layer_count, grid_size = wave_field.shape[1:]
    narrowed = wave_field.astype(jnp.bfloat16)
    products = jnp.dot(
        narrowed.reshape(2 * row_count * layer_count, grid_size),
        dft_table,
        preferred_element_type=jnp.float32,
    )
    products = products.reshape(2, row_count, layer_count, 2, grid_size)
    real_part = products[0, :, :, 0] + products[1, :, :, 1]
    imag_part = products[1, :, :, 0] - products[0, :, :, 1]
    narrowed = jnp.stack([real_part, imag_part]).astype(jnp.bfloat16)
    arrived = lax.all_to_all(narrowed, "plane", split_axis=3, concat_axis=1, tiled=True)
    col_count = arrived.shape[3]
    merged = arrived.reshape(2, grid_size, layer_count * col_count)
    products = jnp.einsum("cxq,xk->cqk", merged, dft_table, preferred_element_type=jnp.float32)
    real_part = products[0, :, :grid_size] + products[1, :, grid_size:]
    imag_part = products[1, :, :grid_size] - products[0, :, grid_size:]
    return jnp.stack([real_part, imag_part]).reshape(2, layer_count, col_count, grid_size)


def inverse(spectrum, dft_table):
    layer_count, col_count, grid_size = spectrum.shape[1:]
    narrowed = spectrum.astype(jnp.bfloat16).reshape(2, layer_count * col_count, grid_size)
    products = jnp.einsum("cqk,kt->ctq", narrowed, dft_table, preferred_element_type=jnp.float32)
    real_part = products[0, :grid_size] - products[1, grid_size:]
    imag_part = products[1, :grid_size] + products[0, grid_size:]
    narrowed = (
        jnp.stack([real_part, imag_part])
        .astype(jnp.bfloat16)
        .reshape(2, grid_size, layer_count, col_count)
    )
    arrived = lax.all_to_all(narrowed, "plane", split_axis=1, concat_axis=3, tiled=True)
    row_count = arrived.shape[1]
    products = jnp.dot(
        arrived.reshape(2 * row_count * layer_count, grid_size),
        dft_table,
        preferred_element_type=jnp.float32,
    )
    products = products.reshape(2, row_count, layer_count, 2, grid_size)
    real_part = products[0, :, :, 0] - products[1, :, :, 1]
    imag_part = products[1, :, :, 0] + products[0, :, :, 1]
    return jnp.stack([real_part, imag_part])


def couple(spectrum, kernel):
    layer_count = spectrum.shape[1]
    real_rows = []
    imag_rows = []
    for out_layer in range(layer_count):
        sum_real = jnp.zeros(spectrum.shape[2:], jnp.float32)
        sum_imag = jnp.zeros(spectrum.shape[2:], jnp.float32)
        for in_layer in range(layer_count):
            kern_real = kernel[0, out_layer, in_layer].astype(jnp.float32)
            kern_imag = kernel[1, out_layer, in_layer].astype(jnp.float32)
            sum_real = (
                sum_real + kern_real * spectrum[0, in_layer] - kern_imag * spectrum[1, in_layer]
            )
            sum_imag = (
                sum_imag + kern_real * spectrum[1, in_layer] + kern_imag * spectrum[0, in_layer]
            )
        real_rows.append(sum_real)
        imag_rows.append(sum_imag)
    return jnp.stack([jnp.stack(real_rows), jnp.stack(imag_rows)])


def green_apply(wave_field, kernel, dft_table):
    return inverse(couple(forward(wave_field, dft_table), kernel), dft_table)


def plain_local(contrast, green_kernel, source_pos, receiver_pos, measured):
    freq_count = green_kernel.shape[0]
    row_count = contrast.shape[1]
    grid_size = contrast.shape[3]
    high = lax.Precision.HIGHEST
    dft_table = phase_tables(grid_size, jnp.bfloat16)
    first_row = lax.axis_index("plane") * row_count
    own_rows = first_row + lax.iota(jnp.int32, row_count)
    all_cols = lax.iota(jnp.int32, grid_size)
    which = 0
    kernel = green_kernel[which]
    phase_y_real, phase_y_imag = line_phase(own_rows, source_pos[which, 1], grid_size)
    phase_x_real, phase_x_imag = line_phase(all_cols, source_pos[which, 0], grid_size)
    source_real = source_gain * (
        phase_y_real[:, None] * phase_x_real[None, :]
        - phase_y_imag[:, None] * phase_x_imag[None, :]
    )
    source_imag = source_gain * (
        phase_y_real[:, None] * phase_x_imag[None, :]
        + phase_y_imag[:, None] * phase_x_real[None, :]
    )
    column_zero = kernel[:, :, 0].astype(jnp.float32)
    spectrum = jnp.stack(
        [
            column_zero[0] * source_real - column_zero[1] * source_imag,
            column_zero[0] * source_imag + column_zero[1] * source_real,
        ]
    )
    incident = inverse(spectrum, dft_table)
    wave_field = incident
    for sweep_index in range(ITERS):
        wave_field = incident + green_apply(
            complex_product(contrast, wave_field), kernel, dft_table
        )
    recv_x = receiver_pos[which, 0]
    recv_y = receiver_pos[which, 1]
    pick_rows = (recv_x[:, None] == own_rows[None, :]).astype(jnp.float32)
    pick_cols = (recv_y[:, None] == all_cols[None, :]).astype(jnp.float32)
    surface = jnp.einsum("rx,cxy->cry", pick_rows, wave_field[:, :, 0, :], precision=high)
    sampled = jnp.sum(surface * pick_cols[None], axis=2)
    gathered = lax.psum(sampled, "plane")
    misfit = gathered - measured[which]
    recv_y_real, recv_y_imag = line_phase(own_rows[None, :], recv_y[:, None], grid_size)
    recv_x_real, recv_x_imag = line_phase(all_cols[None, :], recv_x[:, None], grid_size)
    mixed_real = misfit[0][:, None] * recv_y_real - misfit[1][:, None] * recv_y_imag
    mixed_imag = misfit[0][:, None] * recv_y_imag + misfit[1][:, None] * recv_y_real
    contract = (((0,), (0,)), ((), ()))
    adj_real = lax.dot_general(
        mixed_real, recv_x_real, contract, precision=high, preferred_element_type=jnp.float32
    ) - lax.dot_general(
        mixed_imag, recv_x_imag, contract, precision=high, preferred_element_type=jnp.float32
    )
    adj_imag = lax.dot_general(
        mixed_real, recv_x_imag, contract, precision=high, preferred_element_type=jnp.float32
    ) + lax.dot_general(
        mixed_imag, recv_x_real, contract, precision=high, preferred_element_type=jnp.float32
    )
    row_zero = kernel[:, 0].astype(jnp.float32)
    back_spec = jnp.stack(
        [
            row_zero[0] * adj_real + row_zero[1] * adj_imag,
            row_zero[0] * adj_imag - row_zero[1] * adj_real,
        ]
    )
    backward = inverse(back_spec, dft_table)
    gradient = jnp.stack(
        [
            wave_field[0] * backward[0] + wave_field[1] * backward[1],
            wave_field[0] * backward[1] - wave_field[1] * backward[0],
        ]
    )
    incidents = [incident]
    solutions = [wave_field]
    total_freqs = freq_count * lax.axis_size("freq")
    summed = lax.psum(gradient.astype(jnp.bfloat16), "freq").astype(jnp.float32)
    updated = contrast - summed / total_freqs
    which = 0
    outputs = [
        incidents[which]
        + green_apply(complex_product(updated, solutions[which]), green_kernel[which], dft_table)
    ]
    return (updated, jnp.stack(outputs))


HIGH = lax.Precision.HIGHEST


def fused_kernel(
    cfg, con, kt, cos_t, sin_t, src, rx, ry_real, ry_imag, pick_x, pick_y, meas,
    new_con, new_field,
    tab_a, tab_b, inc, wave, back, vb, spec, hb, send_buf, recv_buf,
    samp_out, samp_in, grad, grad_b, half_in, part_out, part_in, total_b,
    send_sem, recv_sem, samp_send, samp_recv,
    one_send, one_recv, two_send, two_recv, three_send, three_recv, four_send, four_recv,
):
    n, nf, ck, layers = cfg
    wide = 2 * ck
    nz = nf // 2
    me = lax.axis_index("plane")
    fr = lax.axis_index("freq")
    core = fr % 2
    z = fr // 2
    mate = fr + 1 - 2 * core

    def peer(k):
        if n == 4:
            return ((me // 2 + k // 2) % 2) * 2 + (me % 2 + k % 2) % 2
        return (me + k) % n

    def source(k):
        return peer(k) if n == 4 else (me + n - k) % n

    order = [3, 1, 2] if n == 4 else list(range(1, n))
    arrive = [1, 2, 3] if n == 4 else list(range(1, n))
    z_peers = [((z + 1 + j) % nz) * 2 + core for j in range(nz - 1)]

    barrier = pltpu.get_barrier_semaphore()
    for k in range(1, n):
        pl.semaphore_signal(barrier, inc=1, device_id={"plane": peer(k)})
    for dev in z_peers + [mate]:
        pl.semaphore_signal(barrier, inc=1, device_id={"freq": dev})

    def remote(src_ref, dst_ref, s, r, where):
        return pltpu.make_async_remote_copy(
            src_ref=src_ref, dst_ref=dst_ref, send_sem=s, recv_sem=r, device_id=where
        )

    def block(i):
        return pl.ds(pl.multiple_of(i * wide, wide), wide)

    def move(ph, k):
        return remote(
            send_buf.at[ph, k], recv_buf.at[ph, k], send_sem.at[ph, k], recv_sem.at[ph, k],
            {"plane": peer(k)},
        )

    for a in range(n):
        for b in range(n):
            cb = cos_t[a * ck : (a + 1) * ck, b * ck : (b + 1) * ck]
            sb = sin_t[a * ck : (a + 1) * ck, b * ck : (b + 1) * ck]
            r0, c0 = a * wide, b * wide
            for tab, up, down in ((tab_a, -sb, sb), (tab_b, sb, -sb)):
                tab[r0 : r0 + ck, c0 : c0 + ck] = cb
                tab[r0 : r0 + ck, c0 + ck : c0 + wide] = up
                tab[r0 + ck : r0 + wide, c0 : c0 + ck] = down
                tab[r0 + ck : r0 + wide, c0 + ck : c0 + wide] = cb

    def dot(a, b):
        return jnp.dot(a, b, preferred_element_type=jnp.float32)

    def forward(ph):
        def piece(d):
            w = dot(vb[...], tab_a[:, block(d)]).astype(jnp.bfloat16)
            return [
                (c, l, w[l * ck : (l + 1) * ck, c * ck : (c + 1) * ck])
                for c in range(2)
                for l in range(layers)
            ]

        for k in order:
            for c, l, w in piece(peer(k)):
                send_buf[ph, k, c * ck : (c + 1) * ck, l * ck : (l + 1) * ck] = w
            move(ph, k).start()
        for c, l, w in piece(me):
            recv_buf[ph, 0, c * ck : (c + 1) * ck, l * ck : (l + 1) * ck] = w
        spec[...] = dot(tab_b[:, block(me)], recv_buf[ph, 0])
        for k in arrive:
            move(ph, k).wait_recv()
            spec[...] += dot(tab_b[:, block(source(k))], recv_buf[ph, k])
        for k in arrive:
            move(ph, k).wait_send()

    def inverse(ph, dst, base):
        for k in order:
            send_buf[ph, k] = dot(tab_a[block(peer(k)), :], hb[...]).astype(jnp.bfloat16)
            move(ph, k).start()
        recv_buf[ph, 0] = dot(tab_a[block(me), :], hb[...]).astype(jnp.bfloat16)

        def part(k, s):
            p = recv_buf[ph, k]
            lhs = jnp.concatenate(
                [
                    jnp.concatenate(
                        [p[:ck, l * ck : (l + 1) * ck], p[ck:, l * ck : (l + 1) * ck]], axis=1
                    )
                    for l in range(layers)
                ],
                axis=0,
            )
            return dot(lhs, tab_b[block(s), :])

        dst[...] = part(0, me) if base is None else base[...] + part(0, me)
        for k in arrive:
            move(ph, k).wait_recv()
            dst[...] += part(k, source(k))
        for k in arrive:
            move(ph, k).wait_send()

    def multiply(contrast_ref):
        for d in range(n):
            lo = slice(d * wide, d * wide + ck)
            hi = slice(d * wide + ck, (d + 1) * wide)
            a_r, a_i = contrast_ref[:, lo], contrast_ref[:, hi]
            u_r, u_i = wave[:, lo], wave[:, hi]
            vb[:, lo] = (a_r * u_r - a_i * u_i).astype(jnp.bfloat16)
            vb[:, hi] = (a_r * u_i + a_i * u_r).astype(jnp.bfloat16)

    def kern(c, lo, li, g):
        return kt[c, lo, li, g * ck : (g + 1) * ck, :].astype(jnp.float32)

    def put(g, l, real, imag):
        lanes = slice(l * ck, (l + 1) * ck)
        hb[g * wide : g * wide + ck, lanes] = real.astype(jnp.bfloat16)
        hb[g * wide + ck : (g + 1) * wide, lanes] = imag.astype(jnp.bfloat16)

    def couple():
        for g in range(n):
            for lo in range(layers):
                real = imag = None
                for li in range(layers):
                    lanes = slice(li * ck, (li + 1) * ck)
                    f_r = spec[g * wide : g * wide + ck, lanes]
                    f_i = spec[g * wide + ck : (g + 1) * wide, lanes]
                    k_r, k_i = kern(0, lo, li, g), kern(1, lo, li, g)
                    add_r = k_r * f_r - k_i * f_i
                    add_i = k_r * f_i + k_i * f_r
                    real = add_r if real is None else real + add_r
                    imag = add_i if imag is None else imag + add_i
                put(g, lo, real, imag)

    for g in range(n):
        q_r, q_i = src[0, g * ck : (g + 1) * ck, :], src[1, g * ck : (g + 1) * ck, :]
        for l in range(layers):
            k_r, k_i = kern(0, l, 0, g), kern(1, l, 0, g)
            put(g, l, k_r * q_r - k_i * q_i, k_r * q_i + k_i * q_r)

    pl.semaphore_wait(barrier, n - 1 + nz)

    inverse(0, inc, None)
    wave[...] = inc[...]

    def sweep(it, carry):
        multiply(con)
        forward(1 + 2 * it)
        couple()
        inverse(2 + 2 * it, wave, inc)
        return carry

    lax.fori_loop(0, ITERS, sweep, 0)
    ph = 1 + 2 * ITERS

    rows = jnp.dot(pick_x[...], wave[:ck, :], precision=HIGH, preferred_element_type=jnp.float32)
    got_r = got_i = None
    for d in range(n):
        mask = pick_y[:, d * ck : (d + 1) * ck]
        s_r = rows[:, d * wide : d * wide + ck] * mask
        s_i = rows[:, d * wide + ck : (d + 1) * wide] * mask
        got_r = s_r if d == 0 else got_r + s_r
        got_i = s_i if d == 0 else got_i + s_i
    got_r = jnp.sum(got_r, axis=1, keepdims=True)
    got_i = jnp.sum(got_i, axis=1, keepdims=True)
    lane = lax.broadcasted_iota(jnp.int32, samp_out.shape, 1)
    half = samp_out.shape[1] // 2
    samp_out[...] = jnp.where(lane < half, got_r, got_i)

    def tell(k):
        return remote(
            samp_out, samp_in.at[k], samp_send.at[k], samp_recv.at[k], {"plane": peer(k)}
        )

    for k in order:
        tell(k).start()
    misfit = samp_out[...] - meas[...]
    for k in arrive:
        tell(k).wait_recv()
        misfit = misfit + samp_in[k]
    for k in arrive:
        tell(k).wait_send()
    m_r = misfit[:, 0:1]
    m_i = misfit[:, half : half + 1]
    y_r, y_i = ry_real[...], ry_imag[...]
    mixed = jnp.concatenate([m_r * y_r - m_i * y_i, m_r * y_i + m_i * y_r], axis=0)
    for g in range(n):
        adj = jnp.dot(
            rx[g * wide : (g + 1) * wide, :], mixed,
            precision=HIGH, preferred_element_type=jnp.float32,
        )
        a_r, a_i = adj[:ck], adj[ck:]
        for l in range(layers):
            k_r, k_i = kern(0, 0, l, g), kern(1, 0, l, g)
            put(g, l, k_r * a_r + k_i * a_i, k_r * a_i - k_i * a_r)
    inverse(ph, back, None)

    for d in range(n):
        lo = slice(d * wide, d * wide + ck)
        hi = slice(d * wide + ck, (d + 1) * wide)
        b_r, b_i, u_r, u_i = back[:, lo], back[:, hi], wave[:, lo], wave[:, hi]
        g_r = u_r * b_r + u_i * b_i
        g_i = u_r * b_i - u_i * b_r
        grad[:, lo] = g_r
        grad[:, hi] = g_i
        grad_b[:, lo] = g_r.astype(jnp.bfloat16)
        grad_b[:, hi] = g_i.astype(jnp.bfloat16)

    height = grad.shape[0] // 2
    q = height // nz

    def span(c, i):
        return pl.ds(pl.multiple_of(c * height + i * q, q), q)

    def first(j):
        t = (z + 1 + j) % nz
        return remote(
            grad_b.at[span(1 - core, t), :], half_in.at[j],
            one_send.at[j], one_recv.at[j], {"freq": mate},
        )

    def second(j):
        return remote(
            part_out.at[j], part_in.at[j], two_send.at[j], two_recv.at[j], {"freq": z_peers[j]}
        )

    for j in range(nz):
        first(j).start()
    mine = None
    for j in range(nz):
        t = (z + 1 + j) % nz
        first(j).wait_recv()
        mine = grad[span(core, t), :] + half_in[j].astype(jnp.float32)
        if j < nz - 1:
            part_out[j] = mine.astype(jnp.bfloat16)
            second(j).start()
    for j in range(nz - 1):
        second(j).wait_recv()
        mine = mine + part_in[j].astype(jnp.float32)
    total_b[span(core, z), :] = mine.astype(jnp.bfloat16)

    def third(j, i):
        rows_at = total_b.at[span(core, i), :]
        return remote(rows_at, rows_at, three_send.at[j], three_recv.at[j], {"freq": z_peers[j]})

    def fourth(j, c, i):
        rows_at = total_b.at[span(c, i), :]
        return remote(rows_at, rows_at, four_send.at[j], four_recv.at[j], {"freq": mate})

    for j in range(nz - 1):
        third(j, z).start()
    fourth(nz - 1, core, z).start()
    froms = [(z + nz - 1 - j) % nz for j in range(nz - 1)] + [z]
    for j in range(nz - 1):
        third(j, froms[j]).wait_recv()
        fourth(j, core, froms[j]).start()
    for j in reversed(range(nz)):
        fourth(j, 1 - core, froms[j]).wait_recv()
    for j in range(nz):
        first(j).wait_send()
        fourth(j, core, froms[j]).wait_send()
        if j < nz - 1:
            second(j).wait_send()
            third(j, z).wait_send()
    new_con[...] = con[...] - total_b[...].astype(jnp.float32) / nf

    multiply(new_con)
    forward(ph + 1)
    couple()
    inverse(ph + 2, new_field, inc)


def fused_local(contrast, green_kernel, source_pos, receiver_pos, measured):
    _, ck, layers, grid = contrast.shape
    n = lax.axis_size("plane")
    nf = lax.axis_size("freq")
    recv = receiver_pos.shape[2]
    wide = 2 * ck
    pos = np.arange(grid)
    ang = (pos[:, None] * pos[None, :] % grid) * (2.0 * math.pi / grid)
    cos_t = jnp.asarray((np.cos(ang) / math.sqrt(grid)).astype(np.float32).astype(jnp.bfloat16))
    sin_t = jnp.asarray((np.sin(ang) / math.sqrt(grid)).astype(np.float32).astype(jnp.bfloat16))
    own_rows = lax.axis_index("plane") * ck + lax.iota(jnp.int32, ck)
    all_cols = lax.iota(jnp.int32, grid)
    con = contrast.reshape(2, ck, layers, n, ck).transpose(2, 1, 3, 0, 4)
    con = con.reshape(layers * ck, 2 * grid)
    kt = green_kernel[0].transpose(0, 1, 2, 4, 3)
    sy_r, sy_i = line_phase(own_rows, source_pos[0, 1], grid)
    sx_r, sx_i = line_phase(all_cols, source_pos[0, 0], grid)
    src = source_gain * complex_product((sx_r[:, None], sx_i[:, None]), (sy_r[None], sy_i[None]))
    recv_x, recv_y = receiver_pos[0, 0], receiver_pos[0, 1]
    ry_r, ry_i = line_phase(own_rows[None, :], recv_y[:, None], grid)
    rx_r, rx_i = line_phase(all_cols[:, None], recv_x[None, :], grid)
    rx_r, rx_i = rx_r.reshape(n, ck, recv), rx_i.reshape(n, ck, recv)
    rx = jnp.concatenate(
        [jnp.concatenate([rx_r, -rx_i], axis=2), jnp.concatenate([rx_i, rx_r], axis=2)], axis=1
    ).reshape(n * wide, 2 * recv)
    pick_x = (recv_x[:, None] == own_rows[None, :]).astype(jnp.float32)
    pick_y = (recv_y[:, None] == all_cols[None, :]).astype(jnp.float32)
    meas = jnp.repeat(measured[0], 64, axis=0).reshape(2, 64, recv).transpose(2, 0, 1)
    meas = meas.reshape(recv, 128)

    rows, cols, lanes = layers * ck, 2 * grid, layers * ck
    nz = nf // 2
    phases = 2 * ITERS + 4
    f32, bf16 = jnp.float32, jnp.bfloat16
    q = rows // 2 // nz
    dma = pltpu.SemaphoreType.DMA
    vm = pltpu.VMEM
    scratch = [
        vm((cols, cols), bf16), vm((cols, cols), bf16), vm((rows, cols), f32),
        vm((rows, cols), f32), vm((rows, cols), f32), vm((rows, cols), bf16),
        vm((cols, lanes), f32), vm((cols, lanes), bf16),
        vm((phases, n, wide, lanes), bf16), vm((phases, n, wide, lanes), bf16),
        vm((recv, 128), f32), vm((n, recv, 128), f32),
        vm((rows, cols), f32), vm((rows, cols), bf16), vm((nz, q, cols), bf16),
        vm((nz - 1, q, cols), bf16), vm((nz - 1, q, cols), bf16), vm((rows, cols), bf16),
        dma((phases, n)), dma((phases, n)), dma((n,)), dma((n,)),
        dma((nz,)), dma((nz,)), dma((nz - 1,)), dma((nz - 1,)),
        dma((nz - 1,)), dma((nz - 1,)), dma((nz,)), dma((nz,)),
    ]
    spec = pl.BlockSpec(memory_space=pltpu.VMEM)
    new_con, new_field = pl.pallas_call(
        functools.partial(fused_kernel, (n, nf, ck, layers)),
        out_shape=[jax.ShapeDtypeStruct((rows, cols), f32)] * 2,
        in_specs=[spec] * 11,
        out_specs=[spec] * 2,
        scratch_shapes=scratch,
        compiler_params=pltpu.CompilerParams(
            collective_id=0, has_side_effects=True, vmem_limit_bytes=56 * 2**20
        ),
    )(con, kt, cos_t, sin_t, src, rx, ry_r, ry_i, pick_x, pick_y, meas)

    def restore(values):
        values = values.reshape(layers, ck, n, 2, ck).transpose(3, 1, 0, 2, 4)
        return values.reshape(2, ck, layers, grid)

    return restore(new_con), restore(new_field)[None]


def chosen(contrast, green_kernel, source_pos, receiver_pos, measured):
    ck = contrast.shape[1]
    nf = lax.axis_size("freq")
    fits = (
        ck % 128 == 0
        and green_kernel.shape[0] == 1
        and nf % 2 == 0
        and nf >= 4
        and (contrast.shape[2] * ck) % (16 * nf) == 0
        and lax.axis_size("plane") > 1
    )
    body = fused_local if fits else plain_local
    return body(contrast, green_kernel, source_pos, receiver_pos, measured)


def solution(mesh):
    return jax.shard_map(
        chosen,
        mesh=mesh,
        in_specs=(
            P(None, "plane", None, None),
            P("freq", None, None, None, "plane", None),
            P("freq", None),
            P("freq", None, None),
            P("freq", None, None),
        ),
        out_specs=(P(None, "plane", None, None), P("freq", None, "plane", None, None)),
        check_vma=False,
    )
```

profile of v0, /device:TPU:0, one launch (start us, length us, event | category | flops | bytes accessed | tf_op | source)
XLA Modules:
  0.0 124.5 jit_solution(13672509584583910246)
XLA Ops:
  0.7 0.6 copy-done.3
  1.3 0.6 fusion.19
  1.9 0.7 sine_negate_fusion.2
  2.6 0.7 copy-done.5
  3.3 0.7 sine_negate_fusion.1
  4.0 0.7 compare_convert_fusion.pick_x
  4.9 0.7 reshape.280.meas
  5.6 0.8 sine_negate_fusion
  6.4 0.7 fusion.5.pick_y
  7.1 0.2 multiply_subtract_fusion
  7.3 0.8 maximum_multiply_fusion.src
  8.2 1.1 fusion.3
  9.3 1.0 maximum_maximum_fusion
  10.3 1.0 reshape.277
  11.3 0.8 copy.15
  12.2 1.8 %reshape.278.con = f32[256,1024]{1,0:T(8,128)} reshape(f32[2,128,4,2,128]{4,3,2,1,0:T(2,128)S(1)} %bitcast.19) | data formatting | bytes 2097152 | tf_op jit(solution)/shard_map/reshape | solution.py:491
  14.0 1.3 %copy.10 = bf16[1,2,2,2,128,512]{4,5,3,2,1,0:T(8,128)(2,1)} copy(bf16[1,2,2,2,128,512]{5,4,3,2,1,0:T(8,128)(2,1)S(1)} %copy-done.1) | data formatting | bytes 2097152 | tf_op args[1]
  15.3 102.2 %shard_map.86 = (f32[256,1024]{1,0:T(8,128)}, f32[256,1024]{1,0:T(8,128)}) custom-call(f32[256,1024]{1,0:T(8,128)} %reshape.278.con, bf16[2,2,2,512,128]{4,3,2,1,0:T(8,128)(2,1)} %bitcast.18, bf16[512,512]{1,0:T(8,128)(2,1)} %constant.58.clone.cos_t, bf16[512,512]{1,0:T(8,128)(2,1)} %constant.59.clone.sin_t, f32[2,512,128]{2,1,0:T(8,128)} %maximum_multiply_fusion.src, ...), custom_call_target="tpu_custom_call" | custom-call | tf_op jit(solution)/shard_map/pallas_call | solution.py:528
  117.5 2.1 %reshape.281 = f32[2,128,4,2,128]{4,3,2,1,0:T(2,128)S(1)} reshape(f32[256,1024]{1,0:T(8,128)} %get-tuple-element.4) | data formatting | bytes 2097152 | tf_op jit(solution)/shard_map/reshape | solution.py:540
  119.6 0.3 copy.12
  119.9 1.7 %reshape.282 = f32[2,128,2,512]{3,2,1,0:T(2,128)} reshape(f32[2,128,2,4,128]{4,3,2,1,0:T(4,128)S(1)} %copy.12) | data formatting | bytes 2097152 | tf_op jit(solution)/shard_map/reshape | solution.py:541
  121.6 0.9 reshape.283
  122.5 0.3 copy.13
  122.8 1.7 %broadcast_in_dim_reshape.3 = f32[1,2,128,2,512]{4,3,2,1,0:T(2,128)} reshape(f32[2,128,2,4,128]{4,3,2,1,0:T(4,128)S(1)} %copy.13) | data formatting | bytes 2097152 | tf_op jit(solution)/shard_map/broadcast_in_dim;reshape | solution.py:543
  (15 shorter events, 0.3 us)
Async XLA Ops:
  0.6 0.7 copy-start.3
  2.6 0.7 copy-start.5
  4.0 0.7 copy-start.4
  8.2 2.1 %copy-start = (f32[2,128,2,512]{3,2,1,0:T(2,128)S(1)}, f32[2,128,2,512]{3,2,1,0:T(2,128)}, u32[]{:S(2)}) copy-start(f32[2,128,2,512]{3,2,1,0:T(2,128)} %param.7) | copy-start | bytes 3145732
  12.2 1.8 %copy-start.1 = (bf16[1,2,2,2,128,512]{5,4,3,2,1,0:T(8,128)(2,1)S(1)}, bf16[1,2,2,2,128,512]{5,4,3,2,1,0:T(8,128)(2,1)}, u32[]{:S(2)}) copy-start(bf16[1,2,2,2,128,512]{5,4,3,2,1,0:T(8,128)(2,1)} %param.8) | copy-start | bytes 3145732
  119.9 1.8 %copy-start.2 = (f32[256,1024]{1,0:T(8,128)S(1)}, f32[256,1024]{1,0:T(8,128)}, u32[]{:S(2)}) copy-start(f32[256,1024]{1,0:T(8,128)} %get-tuple-element.5) | copy-start | bytes 3145732
where the time goes:
time: 125 us
  Pallas kernels  102 us (82%)
  local copies, waits for them, and re-layouts  14.8 us (12%)
  other arithmetic  6.79 us (5%)
    pallas_call x1, Pallas kernels, fused_local(): pl.pallas_call(functools.partial(fused_kernel, (n, nf, ck, layers)), out_...  102 us
    reshape x2, local copies, waits for them, and re-layouts, restore(): values = values.reshape(layers, ck, n, 2, ck).transpose(3, 1, 0, 2, 4)  3 us
    unnamed x13, local copies, waits for them, and re-layouts  2.63 us

commit v1 on v0

--- a/solution.py
+++ b/solution.py
@@ -195,15 +195,18 @@
 
 
 def fused_kernel(
-    cfg, con, kt, cos_t, sin_t, src, rx, ry_real, ry_imag, pick_x, pick_y, meas,
+    cfg, con_in, kern_in, cos_t, sin_t, src_pos, recv_pos, measured,
     new_con, new_field,
+    con, kt, rx, ry_real, ry_imag, pick_x, pick_y,
     tab_a, tab_b, inc, wave, back, vb, spec, hb, send_buf, recv_buf,
     samp_out, samp_in, grad, grad_b, half_in, part_out, part_in, total_b,
     send_sem, recv_sem, samp_send, samp_recv,
     one_send, one_recv, two_send, two_recv, three_send, three_recv, four_send, four_recv,
 ):
-    n, nf, ck, layers = cfg
+    n, nf, ck, layers, recv = cfg
     wide = 2 * ck
+    length = n * ck
+    quarter = length // 4
     nz = nf // 2
     me = lax.axis_index("plane")
     fr = lax.axis_index("freq")
@@ -257,7 +260,61 @@
     def dot(a, b):
         return jnp.dot(a, b, preferred_element_type=jnp.float32)
 
-    def forward(ph):
+    def turn_cos(turns):
+        x = (turns & (length - 1)).astype(jnp.float32) * (math.pi / length) - math.pi / 2
+        x2 = x * x
+        s = -1.0 / 39916800.0
+        for term in (1.0 / 362880.0, -1.0 / 5040.0, 1.0 / 120.0, -1.0 / 6.0, 1.0):
+            s = term + x2 * s
+        s = x * s
+        return 2.0 * s * s - 1.0
+
+    def iota(shape, axis):
+        return lax.broadcasted_iota(jnp.int32, shape, axis)
+
+    def strided(c, l, d):
+        return pl.ds((c * ck * n + d) * layers + l, ck, stride=n * layers), slice(None)
+
+    def flip(li):
+        for c in range(2):
+            for lo in range(layers):
+                kt[c, lo, li] = kern_in[0, c, lo, li].T
+
+    def prepare():
+        for li in range(1, layers):
+            flip(li)
+        for c in range(2):
+            for l in range(layers):
+                for d in range(n):
+                    at = d * wide + c * ck
+                    con[l * ck : (l + 1) * ck, at : at + ck] = con_in[strided(c, l, d)]
+        eye = iota((recv, recv), 0) == iota((recv, recv), 1)
+
+        def column(row):
+            return jnp.sum(jnp.where(eye, row, 0.0), axis=1, keepdims=True)
+
+        places = recv_pos[0].astype(jnp.float32)
+        x_col, y_col = column(places[0:1]), column(places[1:2])
+        sub, lane = iota((recv, 2 * recv), 0), iota((recv, 2 * recv), 1)
+        both = jnp.where((lane == sub) | (lane == sub + recv), x_col, 0.0)
+        x_row = jnp.sum(both, axis=0, keepdims=True).astype(jnp.int32)
+        x_col, y_col = x_col.astype(jnp.int32), y_col.astype(jnp.int32)
+        late = iota((ck, 2 * recv), 1) >= recv
+        for g in range(n):
+            turns = (g * ck + iota((ck, 2 * recv), 0)) * x_row
+            for c in range(2):
+                shift = jnp.where(late, 0 if c else 3 * quarter, quarter if c else 0)
+                rx[g * wide + c * ck : g * wide + (c + 1) * ck, :] = turn_cos(turns + shift)
+            pick_y[:, g * ck : (g + 1) * ck] = (y_col == g * ck + iota((recv, ck), 1)).astype(
+                jnp.float32
+            )
+        own = me * ck + iota((recv, ck), 1)
+        pick_x[...] = (x_col == own).astype(jnp.float32)
+        ry_real[...] = turn_cos(y_col * own)
+        ry_imag[...] = turn_cos(y_col * own + quarter)
+        return [column(measured[0, c : c + 1, :]) for c in range(2)]
+
+    def forward(ph, beside=None):
         def piece(d):
             w = dot(vb[...], tab_a[:, block(d)]).astype(jnp.bfloat16)
             return [
@@ -273,13 +330,15 @@
         for c, l, w in piece(me):
             recv_buf[ph, 0, c * ck : (c + 1) * ck, l * ck : (l + 1) * ck] = w
         spec[...] = dot(tab_b[:, block(me)], recv_buf[ph, 0])
+        if beside is not None:
+            beside()
         for k in arrive:
             move(ph, k).wait_recv()
             spec[...] += dot(tab_b[:, block(source(k))], recv_buf[ph, k])
         for k in arrive:
             move(ph, k).wait_send()
 
-    def inverse(ph, dst, base):
+    def inverse(ph, dst, base, beside=None):
         for k in order:
             send_buf[ph, k] = dot(tab_a[block(peer(k)), :], hb[...]).astype(jnp.bfloat16)
             move(ph, k).start()
@@ -299,11 +358,13 @@
             return dot(lhs, tab_b[block(s), :])
 
         dst[...] = part(0, me) if base is None else base[...] + part(0, me)
+        kept = beside() if beside is not None else None
         for k in arrive:
             move(ph, k).wait_recv()
             dst[...] += part(k, source(k))
         for k in arrive:
             move(ph, k).wait_send()
+        return kept
 
     def multiply(contrast_ref):
         for d in range(n):
@@ -337,15 +398,19 @@
                     imag = add_i if imag is None else imag + add_i
                 put(g, lo, real, imag)
 
+    flip(0)
     for g in range(n):
-        q_r, q_i = src[0, g * ck : (g + 1) * ck, :], src[1, g * ck : (g + 1) * ck, :]
+        turns = (g * ck + iota((ck, ck), 0)) * src_pos[0, 0]
+        turns = turns + (me * ck + iota((ck, ck), 1)) * src_pos[0, 1]
+        q_r = source_gain * turn_cos(turns)
+        q_i = source_gain * turn_cos(turns + quarter)
         for l in range(layers):
             k_r, k_i = kern(0, l, 0, g), kern(1, l, 0, g)
             put(g, l, k_r * q_r - k_i * q_i, k_r * q_i + k_i * q_r)
 
     pl.semaphore_wait(barrier, n - 1 + nz)
 
-    inverse(0, inc, None)
+    meas_r, meas_i = inverse(0, inc, None, prepare)
     wave[...] = inc[...]
 
     def sweep(it, carry):
@@ -368,9 +433,7 @@
         got_i = s_i if d == 0 else got_i + s_i
     got_r = jnp.sum(got_r, axis=1, keepdims=True)
     got_i = jnp.sum(got_i, axis=1, keepdims=True)
-    lane = lax.broadcasted_iota(jnp.int32, samp_out.shape, 1)
-    half = samp_out.shape[1] // 2
-    samp_out[...] = jnp.where(lane < half, got_r, got_i)
+    samp_out[...] = jnp.where(iota(samp_out.shape, 1) < recv, got_r, got_i)
 
     def tell(k):
         return remote(
@@ -379,14 +442,14 @@
 
     for k in order:
         tell(k).start()
-    misfit = samp_out[...] - meas[...]
+    misfit = samp_out[...]
     for k in arrive:
         tell(k).wait_recv()
         misfit = misfit + samp_in[k]
     for k in arrive:
         tell(k).wait_send()
-    m_r = misfit[:, 0:1]
-    m_i = misfit[:, half : half + 1]
+    m_r = misfit[:, 0:1] - meas_r
+    m_i = misfit[:, recv : recv + 1] - meas_i
     y_r, y_i = ry_real[...], ry_imag[...]
     mixed = jnp.concatenate([m_r * y_r - m_i * y_i, m_r * y_i + m_i * y_r], axis=0)
     for g in range(n):
@@ -467,12 +530,20 @@
         if j < nz - 1:
             second(j).wait_send()
             third(j, z).wait_send()
-    new_con[...] = con[...] - total_b[...].astype(jnp.float32) / nf
-
-    multiply(new_con)
-    forward(ph + 1)
+    con[...] = con[...] - total_b[...].astype(jnp.float32) / nf
+
+    def hand_out(out, values):
+        for c in range(2):
+            for l in range(layers):
+                for d in range(n):
+                    at = d * wide + c * ck
+                    out[strided(c, l, d)] = values[l * ck : (l + 1) * ck, at : at + ck]
+
+    multiply(con)
+    forward(ph + 1, lambda: hand_out(new_con, con))
     couple()
-    inverse(ph + 2, new_field, inc)
+    inverse(ph + 2, back, inc)
+    hand_out(new_field, back)
 
 
 def fused_local(contrast, green_kernel, source_pos, receiver_pos, measured):
@@ -485,25 +556,8 @@
     ang = (pos[:, None] * pos[None, :] % grid) * (2.0 * math.pi / grid)
     cos_t = jnp.asarray((np.cos(ang) / math.sqrt(grid)).astype(np.float32).astype(jnp.bfloat16))
     sin_t = jnp.asarray((np.sin(ang) / math.sqrt(grid)).astype(np.float32).astype(jnp.bfloat16))
-    own_rows = lax.axis_index("plane") * ck + lax.iota(jnp.int32, ck)
-    all_cols = lax.iota(jnp.int32, grid)
-    con = contrast.reshape(2, ck, layers, n, ck).transpose(2, 1, 3, 0, 4)
-    con = con.reshape(layers * ck, 2 * grid)
-    kt = green_kernel[0].transpose(0, 1, 2, 4, 3)
-    sy_r, sy_i = line_phase(own_rows, source_pos[0, 1], grid)
-    sx_r, sx_i = line_phase(all_cols, source_pos[0, 0], grid)
-    src = source_gain * complex_product((sx_r[:, None], sx_i[:, None]), (sy_r[None], sy_i[None]))
-    recv_x, recv_y = receiver_pos[0, 0], receiver_pos[0, 1]
-    ry_r, ry_i = line_phase(own_rows[None, :], recv_y[:, None], grid)
-    rx_r, rx_i = line_phase(all_cols[:, None], recv_x[None, :], grid)
-    rx_r, rx_i = rx_r.reshape(n, ck, recv), rx_i.reshape(n, ck, recv)
-    rx = jnp.concatenate(
-        [jnp.concatenate([rx_r, -rx_i], axis=2), jnp.concatenate([rx_i, rx_r], axis=2)], axis=1
-    ).reshape(n * wide, 2 * recv)
-    pick_x = (recv_x[:, None] == own_rows[None, :]).astype(jnp.float32)
-    pick_y = (recv_y[:, None] == all_cols[None, :]).astype(jnp.float32)
-    meas = jnp.repeat(measured[0], 64, axis=0).reshape(2, 64, recv).transpose(2, 0, 1)
-    meas = meas.reshape(recv, 128)
+    con = contrast.reshape(2, ck, layers, n, ck).transpose(0, 1, 3, 2, 4)
+    con = con.reshape(2 * ck * n * layers, ck)
 
     rows, cols, lanes = layers * ck, 2 * grid, layers * ck
     nz = nf // 2
@@ -513,11 +567,13 @@
     dma = pltpu.SemaphoreType.DMA
     vm = pltpu.VMEM
     scratch = [
+        vm((rows, cols), f32), vm((2, layers, layers, grid, ck), bf16), vm((cols, 2 * recv), f32),
+        vm((recv, ck), f32), vm((recv, ck), f32), vm((recv, ck), f32), vm((recv, grid), f32),
         vm((cols, cols), bf16), vm((cols, cols), bf16), vm((rows, cols), f32),
         vm((rows, cols), f32), vm((rows, cols), f32), vm((rows, cols), bf16),
         vm((cols, lanes), f32), vm((cols, lanes), bf16),
         vm((phases, n, wide, lanes), bf16), vm((phases, n, wide, lanes), bf16),
-        vm((recv, 128), f32), vm((n, recv, 128), f32),
+        vm((recv, 2 * recv), f32), vm((n, recv, 2 * recv), f32),
         vm((rows, cols), f32), vm((rows, cols), bf16), vm((nz, q, cols), bf16),
         vm((nz - 1, q, cols), bf16), vm((nz - 1, q, cols), bf16), vm((rows, cols), bf16),
         dma((phases, n)), dma((phases, n)), dma((n,)), dma((n,)),
@@ -526,18 +582,18 @@
     ]
     spec = pl.BlockSpec(memory_space=pltpu.VMEM)
     new_con, new_field = pl.pallas_call(
-        functools.partial(fused_kernel, (n, nf, ck, layers)),
-        out_shape=[jax.ShapeDtypeStruct((rows, cols), f32)] * 2,
-        in_specs=[spec] * 11,
+        functools.partial(fused_kernel, (n, nf, ck, layers, recv)),
+        out_shape=[jax.ShapeDtypeStruct(con.shape, f32)] * 2,
+        in_specs=[spec] * 4 + [pl.BlockSpec(memory_space=pltpu.SMEM)] + [spec] * 2,
         out_specs=[spec] * 2,
         scratch_shapes=scratch,
         compiler_params=pltpu.CompilerParams(
             collective_id=0, has_side_effects=True, vmem_limit_bytes=56 * 2**20
         ),
-    )(con, kt, cos_t, sin_t, src, rx, ry_r, ry_i, pick_x, pick_y, meas)
+    )(con, green_kernel, cos_t, sin_t, source_pos, receiver_pos, measured)
 
     def restore(values):
-        values = values.reshape(layers, ck, n, 2, ck).transpose(3, 1, 0, 2, 4)
+        values = values.reshape(2, ck, n, layers, ck).transpose(0, 1, 3, 2, 4)
         return values.reshape(2, ck, layers, grid)
 
     return restore(new_con), restore(new_field)[None]
@@ -546,9 +602,12 @@
 def chosen(contrast, green_kernel, source_pos, receiver_pos, measured):
     ck = contrast.shape[1]
     nf = lax.axis_size("freq")
+    grid = contrast.shape[3]
     fits = (
-        ck % 128 == 0
+        ck == 128
         and green_kernel.shape[0] == 1
+        and grid & (grid - 1) == 0
+        and receiver_pos.shape[2] % 64 == 0
         and nf % 2 == 0
         and nf >= 4
         and (contrast.shape[2] * ck) % (16 * nf) == 0

time: 125 us -> 106 us (0.85)
  local copies, waits for them, and re-layouts: 14.8 us -> 3.62 us
  other arithmetic: 6.79 us -> 0 us
    reshape x7 -> x0, local copies, waits for them, and re-layouts: 9.1 us -> none  [the longest x2 3 us: restore(): values = values.reshape(layers, ck, n, 2, ck).transpose(3, 1, 0, 2, 4)]
    neg x3 -> x0, other arithmetic: 2.23 us -> none  [line_phase(): return (jnp.cos(angles), -jnp.sin(angles))]
    another operation x1 -> x0, local copies, waits for them, and re-layouts: 1.75 us -> none  [fused_local(): return (restore(new_con), restore(new_field)[None])]
    convert_element_type x2 -> x0, other arithmetic: 1.4 us -> none  [the longest x1 0.72 us: fused_local(): pick_y = (recv_y[:, None] == all_cols[None, :]).astype(jnp.float32)]
    unnamed x13 -> x4, local copies, waits for them, and re-layouts: 2.63 us -> 3.62 us
where the time goes in v1:
time: 106 us
  Pallas kernels  102 us (96%)
  local copies, waits for them, and re-layouts  3.62 us (3%)
    pallas_call x1, Pallas kernels, fused_local(): pl.pallas_call(functools.partial(fused_kernel, (n, nf, ck, layers, recv))...  102 us
    unnamed x4, local copies, waits for them, and re-layouts  3.62 us

profile of v1, /device:TPU:0, one launch (start us, length us, event | category | flops | bytes accessed | tf_op | source)
XLA Modules:
  0.0 106.3 jit_solution(12945636548904059942)
XLA Ops:
  0.6 102.0 %shard_map.86 = (f32[2048,128]{1,0:T(8,128)}, f32[2048,128]{1,0:T(8,128)}) custom-call(f32[2048,128]{1,0:T(8,128)} %bitcast.15, bf16[1,2,2,2,128,512]{5,4,3,2,1,0:T(8,128)(2,1)} %kern_in.1, bf16[512,512]{1,0:T(8,128)(2,1)} %constant.4.clone.cos_t, bf16[512,512]{1,0:T(8,128)(2,1)} %constant.5.clone.sin_t, s32[1,2]{1,0:T(1,128)} %src_pos.1, ...), custom_call_target="tpu_custom_call" | custom-call | tf_op jit(solution)/shard_map/pallas_call | solution.py:584
  102.6 0.0 copy-start
  102.7 2.6 %copy.14 = f32[2,128,2,512]{3,2,1,0:T(2,128)} copy(f32[2,128,2,512]{3,2,1,0:T(2,128)} %bitcast.17) | data formatting | bytes 2097152
  105.3 0.0 copy-done
  105.3 1.0 copy.15
Async XLA Ops:
  102.6 2.7 %copy-start = (f32[2048,128]{1,0:T(8,128)S(1)}, f32[2048,128]{1,0:T(8,128)}, u32[]{:S(2)}) copy-start(f32[2048,128]{1,0:T(8,128)} %get-tuple-element.5) | copy-start | bytes 3145732
